TPU v7x, 128 devices: a whole 4x4x4 slice. The times are simulated.
128 devices in a mesh: dp: 8 (over x, core), crop: 4 (over y), tensor: 4 (over z).
Axes of the slice: x: 4, y: 4, z: 4, core: 2. Of those that a mesh axis runs over, the one named last changes fastest.
Arguments:
- hidden_a: bfloat16 [2048, 8192], P('crop', 'dp'), as said below
- hidden_b: bfloat16 [2048, 8192], P('crop', 'dp'), as said below
- weight: bfloat16 [8192, 8192], P('dp', 'tensor')
Outputs:
- weight_grad: float32 [8192, 8192], P(('dp', 'crop'), 'tensor')
Inputs may be any that keep to these rules, and one draw needn't show every extreme that they name: `hidden_a`: nonnegative entries. `hidden_b`: nonnegative entries.
All inputs are finite; a program needn't handle non-finite values.
Results may differ from a plain program's by a relative error of at most 0.0015.
Values may be sent and summed in bfloat16 or wider, within the bound.
A program may use at most 128 MiB of HBM per device.

v0:
```python
import jax
import jax.numpy as jnp
from jax import lax
from jax.sharding import PartitionSpec as P

epsilon = 0.0001


def sent_to_all(array, axis):
    peers = lax.axis_size(axis)
    return lax.all_to_all(
        jnp.broadcast_to(array[None], (peers, *array.shape)), axis, 0, 0, tiled=True
    )


def over_copies(array, axis):
    return sent_to_all(array, axis).sum(axis=0)


def body(hidden_a, hidden_b, weight):
    group_size = lax.axis_size(("dp", "crop"))
    data_count = lax.axis_size("dp")
    block_rows = hidden_a.shape[0]
    local_rows = block_rows // data_count
    total_rows = local_rows * group_size
    left_part = jnp.dot(hidden_a, weight, preferred_element_type=jnp.float32)
    right_part = jnp.dot(hidden_b, weight, preferred_element_type=jnp.float32)
    joined = lax.psum_scatter(
        jnp.stack([left_part, right_part], axis=1), "dp", scatter_dimension=0, tiled=True
    ).astype(jnp.bfloat16)
    stacked = jnp.stack([joined[:, 0, :], joined[:, 1, :]]).astype(jnp.float32)
    col_means = over_copies(jnp.sum(stacked, axis=1), ("dp", "crop")) / total_rows
    centered = stacked - col_means[:, None, :]
    spread = over_copies(jnp.sum(centered * centered, axis=1), ("dp", "crop"))
    deviation = jnp.sqrt(spread / (total_rows - 1.0) + epsilon)
    rounded = centered.astype(jnp.bfloat16)
    everyone = lax.all_gather(rounded, ("dp", "crop"), axis=1, tiled=True)
    gram = jnp.einsum("vrf,vbf->vrb", rounded, everyone, preferred_element_type=jnp.float32)
    gram = over_copies(gram, "tensor")
    gram_low = gram.astype(jnp.bfloat16)
    products = jnp.einsum("vrb,vbf->vrf", gram_low, everyone, preferred_element_type=jnp.float32)
    hinge_rate = jnp.where(deviation < 1.0, 25.0 / ((total_rows - 1.0) * deviation), 0.0)[
        :, None, :
    ]
    differ = stacked[0] - stacked[1]
    pull_term = jnp.stack([differ, -differ]) * (50.0 / total_rows)
    cov_scale = 4.0 / (total_rows - 1.0) ** 2
    row_grads = (
        pull_term - hinge_rate * centered + cov_scale * (products - centered * spread[:, None, :])
    )
    row_grads = row_grads.astype(jnp.bfloat16)
    block_grads = lax.all_gather(row_grads, "dp", axis=1, tiled=True)
    across = (((0,), (0,)), ((), ()))
    left_part = lax.dot_general(
        hidden_a, block_grads[0], across, preferred_element_type=jnp.float32
    )
    right_part = lax.dot_general(
        hidden_b, block_grads[1], across, preferred_element_type=jnp.float32
    )
    return lax.psum_scatter(left_part + right_part, "crop", scatter_dimension=0, tiled=True)


def solution(mesh):
    placed = (P("crop", "dp"), P("crop", "dp"), P("dp", "tensor"))
    return jax.shard_map(
        body, mesh=mesh, in_specs=placed, out_specs=P(("dp", "crop"), "tensor"), check_vma=False
    )
```

profile of v0, /device:TPU:1, one launch (start us, length us, event | category | flops | bytes accessed | tf_op | source)
XLA Modules:
  0.0 376.3 jit_solution(18045313686721249146)
XLA Ops:
  6.5 0.0 copy-start
  6.5 0.0 reduce-scatter.3.cloned.1.call-start
  6.5 0.0 copy-start.4
  6.5 5.0 %convolution_bitcast_fusion = f32[512,1,2048]{2,0,1:T(8,128)S(1)} fusion(bf16[512,1024]{1,0:T(8,128)(2,1)} %param.4, bf16[1024,2048]{1,0:T(8,128)(2,1)} %param.5), kind=kOutput, calls=%fused_computation.2 | convolution fusion | flops 2147483648 | bytes 9437184 | tf_op jit(solution)/shard_map/dot_general | solution.py:27
  11.5 0.0 copy-done
  11.5 0.0 copy-done.4
  11.6 2.4 convolution_bitcast_fusion.1
  13.9 3.8 %pad_maximum_fusion = f32[512,2,2048]{2,0,1:T(8,128)} fusion(f32[512,1,2048]{2,0,1:T(8,128)S(1)} %convolution_bitcast_fusion, f32[512,1,2048]{2,0,1:T(8,128)S(1)} %convolution_bitcast_fusion.1), kind=kLoop, calls=%fused_computation | loop fusion | flops 2097152 | bytes 16777216 | tf_op jit(solution)/shard_map/stack | solution.py:29
  17.7 0.0 reduce-scatter.3.cloned.1.call-update
  17.7 0.0 all-gather.3.cloned.1.call-start
  17.8 55.2 %reduce-scatter.3.cloned.1.call-done = f32[64,2,2048]{2,0,1:T(8,128)} async-done(((f32[512,2,2048]{2,0,1:T(8,128)}), f32[64,2,2048]{2,0,1:T(8,128)}) %reduce-scatter.3.cloned.1.call-update) | async-done | bytes 1048592 | tf_op jit(solution)/shard_map/reduce_scatter | solution.py:28
  73.0 1.3 convert_element_type.15
  74.3 0.1 convert_reduce_fusion
  74.4 0.2 broadcast_in_dim.9
  74.7 17.3 %all_to_all.15 = f32[32,2,2048]{2,1,0:T(2,128)S(1)} all-to-all(f32[32,2,2048]{2,1,0:T(2,128)S(1)} %broadcast_in_dim.9), channel_id=1, replica_groups=mesh['dp'=8,'crop'=4,'tensor'=4] {'dp','crop'}, dimensions={0} | all-to-all | bytes 1048576 | tf_op jit(solution)/shard_map/all_to_all | solution.py:11
  92.0 0.2 reduce_sum.46
  92.1 1.0 multiply_reduce_fusion
  93.1 0.0 all-gather.3.cloned.1.call-update
  93.1 1.0 broadcast_in_dim.10
  94.2 4.5 %all-to-all-start.1 = ((f32[32,2,2048]{2,1,0:T(2,128)}), f32[32,2,2048]{2,1,0:T(2,128)S(1)}, u32[]{:S(2)}, u32[]{:S(2)}) async-start(f32[32,2,2048]{2,1,0:T(2,128)} %broadcast_in_dim.10), calls=%async_computation.2 | async-start | bytes 1048576 | tf_op jit(solution)/shard_map/all_to_all | solution.py:11
  98.6 67.9 %all-gather.3.cloned.1.call-done = bf16[2,2048,2048]{2,1,0:T(8,128)(2,1)} async-done(((bf16[2,64,2048]{2,1,0:T(8,128)(2,1)}), bf16[2,2048,2048]{2,1,0:T(8,128)(2,1)}) %all-gather.3.cloned.1.call-update) | async-done | bytes 16777232 | tf_op jit(solution)/shard_map/all_gather | solution.py:37
  166.5 11.1 %fusion.8 = f32[2,64,2048]{2,1,0:T(8,128)S(1)} fusion(bf16[2,64,2048]{2,1,0:T(8,128)(2,1)} %get-tuple-element.8, bf16[2,2048,2048]{2,1,0:T(8,128)(2,1)} %all-gather.3.cloned.1.call-done), kind=kOutput, calls=%fused_computation.25 | convolution fusion | flops 1073741824 | bytes 18350080 | tf_op jit(solution)/shard_map/vrf,vbf->vrb/dot_general | solution.py:38
  177.6 0.0 all-to-all-done.1
  177.6 2.6 broadcast_in_dim.12
  180.2 4.8 %all-to-all-start.2 = ((f32[4,2,64,2048]{3,2,1,0:T(8,128)}), f32[4,2,64,2048]{3,2,1,0:T(8,128)}, u32[]{:S(2)}, u32[]{:S(2)}) async-start(f32[4,2,64,2048]{3,2,1,0:T(8,128)} %broadcast_in_dim.12), calls=%async_computation.3 | async-start | bytes 8388608 | tf_op jit(solution)/shard_map/all_to_all | solution.py:11
  185.0 0.2 all-gather.5.cloned.1.call-start
  185.3 0.1 fusion.6
  185.3 0.9 fusion.7
  186.2 0.2 reduce_sum.48
  186.4 0.0 copy-start.2
  186.5 47.3 %all-to-all-done.2 = f32[4,2,64,2048]{3,2,1,0:T(8,128)} async-done(((f32[4,2,64,2048]{3,2,1,0:T(8,128)}), f32[4,2,64,2048]{3,2,1,0:T(8,128)}, u32[]{:S(2)}, u32[]{:S(2)}) %all-to-all-start.2) | async-done | bytes 4194336 | tf_op jit(solution)/shard_map/all_to_all | solution.py:11
  233.7 2.6 reduce_sum.49
  236.3 0.0 copy-done.2
  236.4 9.8 %fusion.2 = bf16[2,64,2048]{2,1,0:T(8,128)(2,1)} fusion(bf16[2,2048,2048]{2,1,0:T(8,128)(2,1)} %all-gather.3.cloned.1.call-done, f32[1,64,2048]{2,1,0:T(8,128)S(1)} %get-tuple-element.5, f32[1,64,2048]{2,1,0:T(8,128)S(1)} %copy-done.2, f32[2,2048]{1,0:T(2,128)S(1)} %reduce_sum.48, bf16[2,64,2048]{2,1,0:T(8,128)(2,1)S(1)} %reduce_sum.49, ...), kind=kOutput, calls=%fused_computation.7 | convolution fusion | flops 1076887552 | bytes 19447808 | tf_op jit(solution)/shard_map/vrb,vbf->vrf/dot_general | solution.py:41
  246.1 0.0 all-gather.5.cloned.1.call-update
  246.1 0.0 copy-start.3
  246.2 0.0 reduce-scatter.5.cloned.1.call-start
  246.2 30.5 %all-gather.5.cloned.1.call-done = bf16[2,512,2048]{2,1,0:T(8,128)(2,1)} async-done(((bf16[2,64,2048]{2,1,0:T(8,128)(2,1)}), bf16[2,512,2048]{2,1,0:T(8,128)(2,1)}) %all-gather.5.cloned.1.call-update) | async-done | bytes 4194320 | tf_op jit(solution)/shard_map/all_gather | solution.py:52
  276.7 0.0 copy-start.1
  276.7 4.1 %fusion.3 = f32[2048,1024]{1,0:T(8,128)S(1)} fusion(bf16[512,1024]{1,0:T(8,128)(2,1)S(1)} %copy-done, bf16[2,512,2048]{2,1,0:T(8,128)(2,1)} %all-gather.5.cloned.1.call-done), kind=kOutput, calls=%fused_computation.10 | convolution fusion | flops 2147483648 | bytes 11534336 | tf_op jit(solution)/shard_map/dot_general | solution.py:54
  280.8 0.0 copy-done.3
  280.9 0.0 copy-done.1
  280.9 5.8 %add_bitcast_fusion = f32[1024,2048]{0,1:T(8,128)} fusion(f32[2048,1024]{1,0:T(8,128)S(1)} %fusion.3, bf16[512,1024]{1,0:T(8,128)(2,1)S(1)} %copy-done.3, bf16[2,512,2048]{2,1,0:T(8,128)(2,1)S(1)} %copy-done.1), kind=kOutput, calls=%fused_computation.1 | convolution fusion | flops 2149580800 | bytes 19922944 | tf_op jit(solution)/shard_map/dot_general | solution.py:57
  286.7 0.0 reduce-scatter.5.cloned.1.call-update
  286.7 80.2 %reduce-scatter.5.cloned.1.call-done = f32[256,2048]{0,1:T(8,128)} async-done(((f32[1024,2048]{0,1:T(8,128)}), f32[256,2048]{0,1:T(8,128)}) %reduce-scatter.5.cloned.1.call-update) | async-done | bytes 2097168 | tf_op jit(solution)/shard_map/reduce_scatter | solution.py:60
  366.9 2.9 copy.8
  (3 shorter events, 0.1 us)
Async XLA Ops:
  6.5 5.0 %copy-start = (bf16[512,1024]{1,0:T(8,128)(2,1)S(1)}, bf16[512,1024]{1,0:T(8,128)(2,1)}, u32[]{:S(2)}) copy-start(bf16[512,1024]{1,0:T(8,128)(2,1)} %param.3) | copy-start | bytes 3145732
  6.5 66.4 %reduce-scatter.3.cloned.1.call-start = ((), (), s32[]{:S(2)}) async-start(), calls=%async_computation.5 | async-start | bytes 9437184 | tf_op jit(solution)/shard_map/reduce_scatter | solution.py:28
  6.5 5.0 %copy-start.4 = (bf16[1024,2048]{1,0:T(8,128)(2,1)S(1)}, bf16[1024,2048]{1,0:T(8,128)(2,1)}, u32[]{:S(2)}) copy-start(bf16[1024,2048]{1,0:T(8,128)(2,1)} %param.5) | copy-start | bytes 12582916
  17.7 148.7 %all-gather.3.cloned.1.call-start = ((), (), s32[]{:S(2)}) async-start(), calls=%async_computation.6 | async-start | bytes 17301504 | tf_op jit(solution)/shard_map/all_gather | solution.py:37
  94.2 83.5 %all-to-all-start.1 = ((f32[32,2,2048]{2,1,0:T(2,128)}), f32[32,2,2048]{2,1,0:T(2,128)S(1)}, u32[]{:S(2)}, u32[]{:S(2)}) async-start(f32[32,2,2048]{2,1,0:T(2,128)} %broadcast_in_dim.10), calls=%async_computation.2 | async-start | bytes 1048576 | tf_op jit(solution)/shard_map/all_to_all | solution.py:11
  180.2 53.6 %all-to-all-start.2 = ((f32[4,2,64,2048]{3,2,1,0:T(8,128)}), f32[4,2,64,2048]{3,2,1,0:T(8,128)}, u32[]{:S(2)}, u32[]{:S(2)}) async-start(f32[4,2,64,2048]{3,2,1,0:T(8,128)} %broadcast_in_dim.12), calls=%async_computation.3 | async-start | bytes 8388608 | tf_op jit(solution)/shard_map/all_to_all | solution.py:11
  185.0 91.7 %all-gather.5.cloned.1.call-start = ((), (), s32[]{:S(2)}) async-start(), calls=%async_computation.7 | async-start | bytes 4718592 | tf_op jit(solution)/shard_map/all_gather | solution.py:52
  186.4 49.9 %copy-start.2 = (f32[1,64,2048]{2,1,0:T(8,128)S(1)}, f32[1,64,2048]{2,1,0:T(8,128)}, u32[]{:S(2)}) copy-start(f32[1,64,2048]{2,1,0:T(8,128)} %get-tuple-element.6) | copy-start | bytes 1572868
  246.1 34.7 %copy-start.3 = (bf16[512,1024]{1,0:T(8,128)(2,1)S(1)}, bf16[512,1024]{1,0:T(8,128)(2,1)}, u32[]{:S(2)}) copy-start(bf16[512,1024]{1,0:T(8,128)(2,1)} %param.4) | copy-start | bytes 3145732
  246.2 120.7 %reduce-scatter.5.cloned.1.call-start = ((), (), s32[]{:S(2)}) async-start(), calls=%async_computation.8 | async-start | bytes 10485760 | tf_op jit(solution)/shard_map/reduce_scatter | solution.py:60
  276.7 4.2 %copy-start.1 = (bf16[2,512,2048]{2,1,0:T(8,128)(2,1)S(1)}, bf16[2,512,2048]{2,1,0:T(8,128)(2,1)}, u32[]{:S(2)}) copy-start(bf16[2,512,2048]{2,1,0:T(8,128)(2,1)} %all-gather.5.cloned.1.call-done) | copy-start | bytes 12582916
Sparse Core Ops, SparseCore 0:
  17.9 55.0 reduce-scatter.2
  93.2 73.2 all-gather.2
  246.3 30.3 all-gather.4
  286.8 80.0 reduce-scatter.4
where the time goes:
time: 377 us; the launch traced here: 376 us
  waiting for transfers between devices  281 us (75%)
  matrix products  38.2 us (10%)
  blocking collectives  17.3 us (5%)
  between operations  13.3 us (4%)
  other arithmetic  10.1 us (3%)
  starting transfers between devices  9.61 us (3%)
  local copies, waits for them, and re-layouts  6.74 us (2%)
    reduce_scatter x1, waiting for transfers between devices, body(): lax.psum_scatter(left_part + right_part, 'crop', scatter_dimension=0, til...  80.2 us
    all_gather x1, waiting for transfers between devices, body(): everyone = lax.all_gather(rounded, ('dp', 'crop'), axis=1, tiled=True)  67.9 us
    reduce_scatter x1, waiting for transfers between devices, body(): lax.psum_scatter(jnp.stack([left_part, right_part], axis=1), 'dp', scatte...  55.2 us
    all_to_all x2, waiting for transfers between devices, sent_to_all(): lax.all_to_all(jnp.broadcast_to(array[None], (peers, *array.shape)), axis...  47.3 us
    all_gather x1, waiting for transfers between devices, body(): block_grads = lax.all_gather(row_grads, 'dp', axis=1, tiled=True)  30.5 us
    all_to_all x1, blocking collectives, sent_to_all(): lax.all_to_all(jnp.broadcast_to(array[None], (peers, *array.shape)), axis...  17.3 us
    dot_general x1, matrix products, body(): jnp.einsum('vrf,vbf->vrb', rounded, everyone, preferred_element_type=jnp....  11.1 us
    dot_general x1, matrix products, body(): jnp.einsum('vrb,vbf->vrf', gram_low, everyone, preferred_element_type=jnp...  9.76 us
  transfers between devices with their start and end apart: 6, of which 5 were waited for; matrix products, arithmetic and copies ran while one was open for 4% of the time, Pallas kernels for 0%

commit v1 on v0

--- a/solution.py
+++ b/solution.py
@@ -34,7 +34,7 @@
     spread = over_copies(jnp.sum(centered * centered, axis=1), ("dp", "crop"))
     deviation = jnp.sqrt(spread / (total_rows - 1.0) + epsilon)
     rounded = centered.astype(jnp.bfloat16)
-    everyone = lax.all_gather(rounded, ("dp", "crop"), axis=1, tiled=True)
+    everyone = jnp.concatenate(lax.all_gather(rounded, ("dp", "crop")), axis=1)
     gram = jnp.einsum("vrf,vbf->vrb", rounded, everyone, preferred_element_type=jnp.float32)
     gram = over_copies(gram, "tensor")
     gram_low = gram.astype(jnp.bfloat16)

time: 377 us -> 392 us (1.040)
  local copies, waits for them, and re-layouts: 6.74 us -> 22.2 us
    all_gather x0 -> x1, local copies, waits for them, and re-layouts: none -> 14.1 us  [body(): everyone = jnp.concatenate(lax.all_gather(rounded, ('dp', 'crop')), axis=1)]
  transfers between devices with their start and end apart: 6 -> 6, of which waited for: 5 -> 5; matrix products, arithmetic and copies ran while one was open for 4% -> 7% of each run, Pallas kernels for 0% -> 0%
where the time goes in v1:
time: 392 us; the launch traced here: 391 us
  waiting for transfers between devices  281 us (72%)
  matrix products  37.7 us (10%)
  local copies, waits for them, and re-layouts  22.2 us (6%)
  blocking collectives  17.3 us (4%)
  between operations  13.3 us (3%)
  other arithmetic  10.2 us (3%)
  starting transfers between devices  9.61 us (2%)
    reduce_scatter x1, waiting for transfers between devices, body(): lax.psum_scatter(left_part + right_part, 'crop', scatter_dimension=0, til...  80.2 us
    all_gather x1, waiting for transfers between devices, body(): everyone = jnp.concatenate(lax.all_gather(rounded, ('dp', 'crop')), axis=1)  67.5 us
    reduce_scatter x1, waiting for transfers between devices, body(): lax.psum_scatter(jnp.stack([left_part, right_part], axis=1), 'dp', scatte...  55.2 us
    all_to_all x2, waiting for transfers between devices, sent_to_all(): lax.all_to_all(jnp.broadcast_to(array[None], (peers, *array.shape)), axis...  47.3 us
    all_gather x1, waiting for transfers between devices, body(): block_grads = lax.all_gather(row_grads, 'dp', axis=1, tiled=True)  30.5 us
    all_to_all x1, blocking collectives, sent_to_all(): lax.all_to_all(jnp.broadcast_to(array[None], (peers, *array.shape)), axis...  17.3 us
    all_gather x1, local copies, waits for them, and re-layouts, body(): everyone = jnp.concatenate(lax.all_gather(rounded, ('dp', 'crop')), axis=1)  14.1 us
    dot_general x1, matrix products, body(): jnp.einsum('vrf,vbf->vrb', rounded, everyone, preferred_element_type=jnp....  10.9 us
  transfers between devices with their start and end apart: 6, of which 5 were waited for; matrix products, arithmetic and copies ran while one was open for 7% of the time, Pallas kernels for 0%

profile of v1, /device:TPU:1, one launch (start us, length us, event | category | flops | bytes accessed | tf_op | source)
XLA Modules:
  0.0 391.0 jit_solution(15544803667763539559)
XLA Ops:
  6.5 0.0 copy-start
  6.5 0.0 copy-start.3
  6.5 0.0 reduce-scatter.3.cloned.1.call-start
  6.5 1.2 copy-done
  7.8 4.7 %convolution_bitcast_fusion.1 = f32[512,1,2048]{2,0,1:T(8,128)S(1)} fusion(bf16[512,1024]{1,0:T(8,128)(2,1)S(1)} %copy-done, bf16[1024,2048]{1,0:T(8,128)(2,1)} %param.5), kind=kOutput, calls=%fused_computation.3 | convolution fusion | flops 2147483648 | bytes 9437184 | tf_op jit(solution)/shard_map/dot_general | solution.py:26
  12.4 0.0 copy-done.3
  12.4 0.0 copy-done.5
  12.5 2.4 convolution_bitcast_fusion
  14.8 3.8 pad_maximum_fusion
  18.6 0.0 reduce-scatter.3.cloned.1.call-update
  18.7 0.0 all-gather.3.cloned.1.call-start
  18.7 55.2 %reduce-scatter.3.cloned.1.call-done = f32[64,2,2048]{2,0,1:T(8,128)} async-done(((f32[512,2,2048]{2,0,1:T(8,128)}), f32[64,2,2048]{2,0,1:T(8,128)}) %reduce-scatter.3.cloned.1.call-update) | async-done | bytes 1048592 | tf_op jit(solution)/shard_map/reduce_scatter | solution.py:28
  73.9 1.3 convert_element_type.33
  75.2 0.1 slice_bitcast_fusion.7
  75.3 0.1 convert_reduce_fusion
  75.4 0.2 broadcast_in_dim.9
  75.7 17.3 %all_to_all.15 = f32[32,2,2048]{2,1,0:T(2,128)S(1)} all-to-all(f32[32,2,2048]{2,1,0:T(2,128)S(1)} %broadcast_in_dim.9), channel_id=1, replica_groups=mesh['dp'=8,'crop'=4,'tensor'=4] {'dp','crop'}, dimensions={0} | all-to-all | bytes 1048576 | tf_op jit(solution)/shard_map/all_to_all | solution.py:11
  93.0 0.2 reduce_sum.46
  93.1 0.9 subtract_convert_fusion
  94.0 0.0 all-gather.3.cloned.1.call-update
  94.1 0.2 multiply_reduce_fusion
  94.2 1.0 broadcast_in_dim.10
  95.3 4.5 %all-to-all-start.1 = ((f32[32,2,2048]{2,1,0:T(2,128)}), f32[32,2,2048]{2,1,0:T(2,128)S(1)}, u32[]{:S(2)}, u32[]{:S(2)}) async-start(f32[32,2,2048]{2,1,0:T(2,128)} %broadcast_in_dim.10), calls=%async_computation.2 | async-start | bytes 1048576 | tf_op jit(solution)/shard_map/all_to_all | solution.py:11
  99.8 67.5 %all-gather.3.cloned.1.call-done = bf16[32,2,64,2048]{3,2,1,0:T(8,128)(2,1)} async-done(((bf16[1,2,64,2048]{3,2,1,0:T(8,128)(2,1)}), bf16[32,2,64,2048]{3,2,1,0:T(8,128)(2,1)}) %all-gather.3.cloned.1.call-update) | async-done | bytes 16777232 | tf_op jit(solution)/shard_map/all_gather | solution.py:37
  167.3 14.1 %copy.13 = bf16[32,2,64,2048]{3,2,0,1:T(8,128)(2,1)} copy(bf16[32,2,64,2048]{3,2,1,0:T(8,128)(2,1)} %all-gather.3.cloned.1.call-done) | data formatting | bytes 33554432 | tf_op jit(solution)/shard_map/all_gather | solution.py:37
  181.4 10.9 %fusion.5 = f32[2,64,2048]{2,1,0:T(8,128)S(1)} fusion(bf16[2,2048,2048]{2,1,0:T(8,128)(2,1)} %bitcast.32, f32[2,2048]{1,0:T(2,128)S(1)} %broadcast_multiply_fusion, bf16[1,64,2048]{2,1,0:T(8,128)(2,1)S(1)} %get-tuple-element.10, bf16[1,64,2048]{2,1,0:T(8,128)(2,1)S(1)} %get-tuple-element.7), kind=kOutput, calls=%fused_computation.17 | convolution fusion | flops 1074790400 | bytes 18366464 | tf_op jit(solution)/shard_map/vrf,vbf->vrb/dot_general | solution.py:38
  192.3 0.0 all-to-all-done.1
  192.3 2.6 broadcast_in_dim.12
  194.9 4.8 %all-to-all-start.2 = ((f32[4,2,64,2048]{3,2,1,0:T(8,128)}), f32[4,2,64,2048]{3,2,1,0:T(8,128)}, u32[]{:S(2)}, u32[]{:S(2)}) async-start(f32[4,2,64,2048]{3,2,1,0:T(8,128)} %broadcast_in_dim.12), calls=%async_computation.3 | async-start | bytes 8388608 | tf_op jit(solution)/shard_map/all_to_all | solution.py:11
  199.7 0.2 all-gather.5.cloned.1.call-start
  200.0 0.1 fusion.8
  200.1 0.9 fusion.9
  201.0 0.2 reduce_sum.48
  201.2 47.3 %all-to-all-done.2 = f32[4,2,64,2048]{3,2,1,0:T(8,128)} async-done(((f32[4,2,64,2048]{3,2,1,0:T(8,128)}), f32[4,2,64,2048]{3,2,1,0:T(8,128)}, u32[]{:S(2)}, u32[]{:S(2)}) %all-to-all-start.2) | async-done | bytes 4194336 | tf_op jit(solution)/shard_map/all_to_all | solution.py:11
  248.4 2.6 reduce_sum.49
  251.1 0.0 copy-done.2
  251.1 9.8 %fusion.2 = bf16[2,64,2048]{2,1,0:T(8,128)(2,1)} fusion(bf16[2,2048,2048]{2,1,0:T(8,128)(2,1)} %bitcast.33, f32[1,64,2048]{2,1,0:T(8,128)S(1)} %get-tuple-element.5, f32[1,64,2048]{2,1,0:T(8,128)S(1)} %copy-done.2, f32[2,2048]{1,0:T(2,128)S(1)} %reduce_sum.48, bf16[2,64,2048]{2,1,0:T(8,128)(2,1)S(1)} %reduce_sum.49, f32[2,2048]{1,0:T(2,128)S(1)} %compare_select_fusion, ...), kind=kOutput, calls=%fused_computation.7 | convolution fusion | flops 1076887552 | bytes 19447808 | tf_op jit(solution)/shard_map/vrb,vbf->vrf/dot_general | solution.py:41
  260.8 0.0 all-gather.5.cloned.1.call-update
  260.8 0.0 copy-start.4
  260.9 0.0 reduce-scatter.5.cloned.1.call-start
  260.9 30.5 %all-gather.5.cloned.1.call-done = bf16[2,512,2048]{2,1,0:T(8,128)(2,1)} async-done(((bf16[2,64,2048]{2,1,0:T(8,128)(2,1)}), bf16[2,512,2048]{2,1,0:T(8,128)(2,1)}) %all-gather.5.cloned.1.call-update) | async-done | bytes 4194320 | tf_op jit(solution)/shard_map/all_gather | solution.py:52
  291.4 4.1 %fusion.3 = f32[2048,1024]{1,0:T(8,128)S(1)} fusion(bf16[512,1024]{1,0:T(8,128)(2,1)S(1)} %copy-done, bf16[2,512,2048]{2,1,0:T(8,128)(2,1)} %all-gather.5.cloned.1.call-done), kind=kOutput, calls=%fused_computation.10 | convolution fusion | flops 2147483648 | bytes 11534336 | tf_op jit(solution)/shard_map/dot_general | solution.py:54
  295.6 0.0 copy-done.4
  295.6 0.0 copy-done.1
  295.6 5.8 %add_bitcast_fusion = f32[1024,2048]{0,1:T(8,128)} fusion(f32[2048,1024]{1,0:T(8,128)S(1)} %fusion.3, bf16[512,1024]{1,0:T(8,128)(2,1)S(1)} %copy-done.4, bf16[2,512,2048]{2,1,0:T(8,128)(2,1)S(1)} %copy-done.1), kind=kOutput, calls=%fused_computation.1 | convolution fusion | flops 2149580800 | bytes 19922944 | tf_op jit(solution)/shard_map/dot_general | solution.py:57
  301.4 0.0 reduce-scatter.5.cloned.1.call-update
  301.4 80.2 %reduce-scatter.5.cloned.1.call-done = f32[256,2048]{0,1:T(8,128)} async-done(((f32[1024,2048]{0,1:T(8,128)}), f32[256,2048]{0,1:T(8,128)}) %reduce-scatter.5.cloned.1.call-update) | async-done | bytes 2097168 | tf_op jit(solution)/shard_map/reduce_scatter | solution.py:60
  381.6 2.9 copy.14
  (5 shorter events, 0.1 us)
Async XLA Ops:
  6.5 1.2 copy-start
  6.5 5.9 %copy-start.3 = (bf16[512,1024]{1,0:T(8,128)(2,1)S(1)}, bf16[512,1024]{1,0:T(8,128)(2,1)}, u32[]{:S(2)}) copy-start(bf16[512,1024]{1,0:T(8,128)(2,1)} %param.4) | copy-start | bytes 3145732
  6.5 67.4 %reduce-scatter.3.cloned.1.call-start = ((), (), s32[]{:S(2)}) async-start(), calls=%async_computation.5 | async-start | bytes 9437184 | tf_op jit(solution)/shard_map/reduce_scatter | solution.py:28
  7.8 4.7 %copy-start.5 = (bf16[1024,2048]{1,0:T(8,128)(2,1)S(1)}, bf16[1024,2048]{1,0:T(8,128)(2,1)}, u32[]{:S(2)}) copy-start(bf16[1024,2048]{1,0:T(8,128)(2,1)} %param.5) | copy-start | bytes 12582916
  18.7 148.6 %all-gather.3.cloned.1.call-start = ((), (), s32[]{:S(2)}) async-start(), calls=%async_computation.6 | async-start | bytes 17301504 | tf_op jit(solution)/shard_map/all_gather | solution.py:37
  95.3 97.1 %all-to-all-start.1 = ((f32[32,2,2048]{2,1,0:T(2,128)}), f32[32,2,2048]{2,1,0:T(2,128)S(1)}, u32[]{:S(2)}, u32[]{:S(2)}) async-start(f32[32,2,2048]{2,1,0:T(2,128)} %broadcast_in_dim.10), calls=%async_computation.2 | async-start | bytes 1048576 | tf_op jit(solution)/shard_map/all_to_all | solution.py:11
  194.9 53.5 %all-to-all-start.2 = ((f32[4,2,64,2048]{3,2,1,0:T(8,128)}), f32[4,2,64,2048]{3,2,1,0:T(8,128)}, u32[]{:S(2)}, u32[]{:S(2)}) async-start(f32[4,2,64,2048]{3,2,1,0:T(8,128)} %broadcast_in_dim.12), calls=%async_computation.3 | async-start | bytes 8388608 | tf_op jit(solution)/shard_map/all_to_all | solution.py:11
  199.7 91.7 %all-gather.5.cloned.1.call-start = ((), (), s32[]{:S(2)}) async-start(), calls=%async_computation.7 | async-start | bytes 4718592 | tf_op jit(solution)/shard_map/all_gather | solution.py:52
  201.1 49.9 %copy-start.2 = (f32[1,64,2048]{2,1,0:T(8,128)S(1)}, f32[1,64,2048]{2,1,0:T(8,128)}, u32[]{:S(2)}) copy-start(f32[1,64,2048]{2,1,0:T(8,128)} %get-tuple-element.6) | copy-start | bytes 1572868
  260.8 34.7 %copy-start.4 = (bf16[512,1024]{1,0:T(8,128)(2,1)S(1)}, bf16[512,1024]{1,0:T(8,128)(2,1)}, u32[]{:S(2)}) copy-start(bf16[512,1024]{1,0:T(8,128)(2,1)} %param.4) | copy-start | bytes 3145732
  260.9 120.8 %reduce-scatter.5.cloned.1.call-start = ((), (), s32[]{:S(2)}) async-start(), calls=%async_computation.8 | async-start | bytes 10485760 | tf_op jit(solution)/shard_map/reduce_scatter | solution.py:60
  291.4 4.2 %copy-start.1 = (bf16[2,512,2048]{2,1,0:T(8,128)(2,1)S(1)}, bf16[2,512,2048]{2,1,0:T(8,128)(2,1)}, u32[]{:S(2)}) copy-start(bf16[2,512,2048]{2,1,0:T(8,128)(2,1)} %all-gather.5.cloned.1.call-done) | copy-start | bytes 12582916
Sparse Core Ops, SparseCore 0:
  18.8 55.0 reduce-scatter.2
  94.2 73.0 all-gather.2
  261.0 30.3 all-gather.4
  301.5 80.0 reduce-scatter.4
